TPU v7x, 32 devices: a 4x2x2 block of a 4x4x8 slice. The times are simulated.
32 devices in a mesh: dp: 4 (over y, z), tp: 8 (over x, core).
Axes of the slice: x: 4, y: 2, z: 2, core: 2. Of those that a mesh axis runs over, the one named last changes fastest.
The devices are a block of a 4x4x8 slice.
Arguments:
- x: bfloat16 [4, 2048, 1024], P('dp', 'tp'), parts along dimension 0
- ln1_gamma: float32 [1024], replicated
- ln1_beta: float32 [1024], replicated
- w_qkv: bfloat16 [1024, 16, 3, 64], P(None, 'tp')
- b_qkv: float32 [16, 3, 64], P('tp')
- w_out: bfloat16 [1024, 1024], P('tp')
- b_out: float32 [1024], replicated
- ln2_gamma: float32 [1024], replicated
- ln2_beta: float32 [1024], replicated
- w_up: bfloat16 [1024, 4096], P(None, 'tp')
- b_up: float32 [4096], P('tp')
- w_down: bfloat16 [4096, 1024], P('tp')
- b_down: float32 [1024], replicated
- grad_y: bfloat16 [4, 2048, 1024], P('dp', 'tp'), parts along dimension 0
Outputs:
- output 1: bfloat16 [4, 2048, 1024], P('dp', 'tp'), parts along dimension 0
- output 2: bfloat16 [4, 2048, 1024], P('dp', 'tp'), parts along dimension 0
- output 3: float32 [4096], P('dp'), parts along dimension 0
- output 4: float32 [4096], P('dp'), parts along dimension 0
- output 5: bfloat16 [4096, 16, 3, 64], P('dp', 'tp'), parts along dimension 0
- output 6: float32 [64, 3, 64], P(('dp', 'tp')), parts along dimension 0
- output 7: bfloat16 [4096, 1024], P(('dp', 'tp')), parts along dimension 0
- output 8: float32 [4096], P('dp'), parts along dimension 0
- output 9: float32 [4096], P('dp'), parts along dimension 0
- output 10: float32 [4096], P('dp'), parts along dimension 0
- output 11: bfloat16 [4096, 4096], P('dp', 'tp'), parts along dimension 0
- output 12: float32 [16384], P(('dp', 'tp')), parts along dimension 0
- output 13: bfloat16 [16384, 1024], P(('dp', 'tp')), parts along dimension 0
- output 14: float32 [4096], P('dp'), parts along dimension 0
There are 4 independent parts. A program takes and returns all parts, laid end to end along the dimension named above; an argument that names none is the same for every part.
All inputs are finite; a program needn't handle non-finite values.
Results may differ from a plain program's by a relative error of at most 0.02.
Values are sent between devices in bfloat16 or wider.
A program may use at most 768 MiB of HBM per device.

v0:
```python
import functools
import math
import jax
import jax.numpy as jnp
import numpy as np
from jax import lax
from jax.experimental import pallas as pl
from jax.experimental.pallas import tpu as pltpu
from jax.sharding import PartitionSpec as P

EPS = 1e-5
MASK_VALUE = -1e30
BF, F32 = jnp.bfloat16, jnp.float32
VMEM = pltpu.VMEM
MESH = pl.DeviceIdType.MESH
scope = jax.named_scope
VLIM = 58 * 1024 * 1024
GELU_C = math.sqrt(2.0 / math.pi)
PAIR = LOW, HIGH = (0, 1)
TRIPLE = (0, 1, 2)
NN = (((1,), (0,)), ((), ()))
T0 = (((0,), (0,)), ((), ()))
NT = (((1,), (1,)), ((), ()))


def alibi_slopes(n_heads):
    closest = 2 ** int(math.floor(math.log2(n_heads)))
    base_ratio = 2.0 ** (-8.0 / closest)
    extra_ratio = 2.0 ** (-4.0 / closest)
    remaining = min(closest, n_heads - closest)
    slopes = [base_ratio ** (i + 1) for i in range(closest)]
    slopes = slopes + [extra_ratio ** (2 * i + 1) for i in range(remaining)]
    return np.array(slopes, dtype=np.float32)


def mm(a, b, dims=NN):
    return lax.dot_general(a, b, dims, preferred_element_type=F32)


def loop(lo, hi, body, unroll=1):
    def step(i, carry):
        body(i)
        return carry
    lax.fori_loop(lo, hi, step, 0, unroll=unroll)


def twos(count, body):
    loop(0, count // 2, lambda i: body((2 * i, 2 * i + 1)))

    @pl.when(count % 2 == 1)
    def _():
        body((count - 1,))


def rows_loop(total, rows, body, base=0):
    loop(0, total // rows, lambda r: body(pl.ds(pl.multiple_of(base + r * rows, rows), rows)))


def row_mean(z):
    return jnp.mean(z, axis=-1, keepdims=True)


def col_sum(z):
    return jnp.sum(z, axis=0, keepdims=True)


def norm_back(grad, hat, rstd):
    return rstd * (grad - row_mean(grad) - hat * row_mean(grad * hat))


def zero_fill(*refs):
    for ref in refs:
        ref[...] = jnp.zeros(ref.shape, ref.dtype)


def sort_weight(wp, wt):
    e = wp.shape[0] // 6
    for part_no in TRIPLE:
        for head in PAIR:
            dst = (part_no * 2 + head) * e
            src = (head * 3 + part_no) * e
            wp[dst:dst + e, :] = wt[src:src + e, :]


def norm_rows(z):
    cen = z - row_mean(z)
    rstd = lax.rsqrt(row_mean(cen * cen) + EPS)
    return cen * rstd, rstd


def fold8(v, op):
    out = v[0:8]
    for k in range(1, v.shape[0] // 8):
        out = op(out, v[8 * k:8 * k + 8])
    return out


class Ring:
    def __init__(self, n):
        self.n = n
        nx = n // 2
        self.me = lax.axis_index('tp')
        self.x = self.me // 2
        self.c = self.me % 2
        self.nx = nx
        self.xr = (self.x + 1) % nx
        self.xl = (self.x + nx - 1) % nx
        self.xf = (self.x + 2) % nx
        self.right = self.xr * 2 + self.c
        self.left = self.xl * 2 + self.c
        self.far = self.xf * 2 + self.c
        other = 1 - self.c
        self.partner = self.x * 2 + other
        self.others = [xp * 2 + other for xp in (self.x, self.xl, self.xr, self.xf)]

    def order(self, s):
        odd = s % 2
        dx = jnp.where(s < 2, 0, jnp.where(s >= 6, 2, jnp.where(odd == 0, self.nx - 1, 1)))
        mid = jnp.where(s < 4, 0, 1)
        dc = jnp.where(s < 2, odd, jnp.where(s >= 6, odd, mid))
        return ((self.x + dx) % self.nx) * 2 + (self.c + dc) % 2

    def barrier(self):
        sem = pltpu.get_barrier_semaphore()
        peers = [self.right, self.left, self.partner]
        for peer in peers:
            pl.semaphore_signal(sem, inc=1, device_id={'tp': peer}, device_id_type=MESH)
        pl.semaphore_wait(sem, len(peers))


class Gather:
    LEFT, RIGHT, FAR, SIDE = 0, 2, 4, 6
    SLOTS = 10

    def __init__(self, ring, buf, ssem, rsem, base=0, size=None, cut=None):
        self.ring, self.buf, self.ssem, self.rsem = ring, buf, ssem, rsem
        self.base = base
        self.size = size or buf.shape[1]
        self.cut = cut or self.size // 2
        self.drained = False

    def rows(self, half):
        if half == LOW:
            return pl.ds(self.base, self.cut)
        return pl.ds(self.base + self.cut, self.size - self.cut)

    def copy(self, ref, dev, slot, onward):
        return pltpu.make_async_remote_copy(
            src_ref=ref, dst_ref=ref, send_sem=self.ssem.at[onward], recv_sem=self.rsem.at[slot],
            device_id={'tp': dev}, device_id_type=MESH)

    def send(self, blk, half, dev, slot, onward=LOW):
        self.copy(self.buf.at[blk, self.rows(half)], dev, slot, onward).start()

    def wait(self, blk, half, slot):
        self.copy(self.buf.at[blk, self.rows(half)], self.ring.me, slot, LOW).wait_recv()

    def side(self, which):
        ref = self.buf.at[self.ring.others[which], pl.ds(self.base, self.size)]
        self.copy(ref, self.ring.me, self.SIDE + which, LOW).wait_recv()

    def start(self):
        r = self.ring
        for half in PAIR:
            self.send(r.me, half, r.right, self.LEFT + half)
            self.send(r.me, HIGH - half, r.left, self.RIGHT + HIGH - half)
        for half in PAIR:
            self.send(r.me, half, r.partner, self.SIDE)

    def near1(self):
        r = self.ring
        self.wait(r.left, LOW, self.LEFT)
        self.send(r.left, LOW, r.right, self.FAR, HIGH)
        self.send(r.left, LOW, r.partner, self.SIDE + 1)
        self.wait(r.right, HIGH, self.RIGHT + HIGH)
        self.send(r.right, HIGH, r.left, self.FAR + HIGH, HIGH)
        self.send(r.right, HIGH, r.partner, self.SIDE + 2)

    def near2(self):
        r = self.ring
        self.wait(r.left, HIGH, self.LEFT + HIGH)
        self.send(r.left, HIGH, r.partner, self.SIDE + 1)
        self.wait(r.right, LOW, self.RIGHT)
        self.send(r.right, LOW, r.partner, self.SIDE + 2)

    def far(self):
        r = self.ring
        for half in PAIR:
            self.wait(r.far, half, self.FAR + half)
            self.send(r.far, half, r.partner, self.SIDE + 3)

    def gone(self, blocks, onward):
        ref = self.buf.at[pl.ds(0, blocks), pl.ds(self.base, self.size)]
        self.copy(ref, self.ring.right, LOW, onward).wait_send()

    def drain(self):
        self.gone(1, HIGH)
        self.drained = True

    def finish(self):
        self.gone(6, LOW)
        if not self.drained:
            self.gone(1, HIGH)


class Scatter:
    def __init__(self, ring, part, pair, stage, land, ssem, rsem, base=0, size=None):
        self.ring, self.part, self.pair, self.stage, self.land = ring, part, pair, stage, land
        self.ssem, self.rsem = ssem, rsem
        self.base = base
        self.size = size or part.shape[1]
        self.half = self.size // 2

    def cp_pair(self, xp):
        r = self.ring
        rows = pl.ds(self.base, self.size)
        return pltpu.make_async_remote_copy(
            src_ref=self.part.at[xp * 2 + (1 - r.c), rows], dst_ref=self.pair.at[xp, rows], send_sem=self.ssem.at[LOW],
            recv_sem=self.rsem.at[xp], device_id={'tp': r.partner}, device_id_type=MESH)

    def cp(self, slot, half, dst_slot, dev):
        rows = pl.ds(self.base + half * self.half, self.half)
        return pltpu.make_async_remote_copy(
            src_ref=self.stage.at[slot, rows], dst_ref=self.land.at[dst_slot, rows],
            send_sem=self.ssem.at[HIGH], recv_sem=self.rsem.at[4 + 2 * dst_slot + half],
            device_id={'tp': dev}, device_id_type=MESH)

    def wait_land(self, dst_slot, half):
        self.cp(0, half, dst_slot, self.ring.me).wait_recv()

    def wait_pair(self, xp):
        self.cp_pair(xp).wait_recv()

    def send_pair(self, xp):
        self.cp_pair(xp).start()

    def mix(self, slot, xp, half, with_far=False):
        blk = xp * 2 + self.ring.c
        step = 32

        def body(i):
            rows = pl.ds(pl.multiple_of(self.base + half * self.half + i * step, step), step)
            total = self.part[blk, rows, :].astype(F32) + self.pair[xp, rows, :].astype(F32)
            if with_far:
                total = total + self.land[0, rows, :].astype(F32)
            self.stage[slot, rows, :] = total.astype(BF)
        loop(0, self.half // step, body)

    def far(self):
        r = self.ring
        self.wait_pair(r.xf)
        self.mix(0, r.xf, 0)
        self.cp(0, 0, 0, r.right).start()
        self.mix(0, r.xf, 1)
        self.cp(0, 1, 0, r.left).start()

    def near_own(self):
        r = self.ring
        self.wait_pair(r.xr)
        self.mix(1, r.xr, 1)
        self.cp(1, 1, 1, r.right).start()
        self.wait_pair(r.xl)
        self.mix(2, r.xl, 0)
        self.cp(2, 0, 2, r.left).start()

    def near_sum(self):
        r = self.ring
        self.wait_land(0, 0)
        self.mix(1, r.xr, 0, with_far=True)
        self.cp(1, 0, 1, r.right).start()
        self.wait_land(0, 1)
        self.mix(2, r.xl, 1, with_far=True)
        self.cp(2, 1, 2, r.left).start()

    def wait_final(self):
        self.wait_pair(self.ring.x)
        for slot in (1, 2):
            for half in PAIR:
                self.wait_land(slot, half)

    def total(self, rows):
        r = self.ring
        return (self.part[r.me, rows, :].astype(F32) + self.pair[r.x, rows, :].astype(F32)
                + self.land[1, rows, :].astype(F32) + self.land[2, rows, :].astype(F32))

    def finish(self):
        r = self.ring
        rows = pl.ds(self.base, self.size)
        for ref, which in ((self.pair.at[:, rows], LOW), (self.stage.at[:, rows], HIGH)):
            pltpu.make_async_remote_copy(
                src_ref=ref, dst_ref=ref, send_sem=self.ssem.at[which], recv_sem=self.rsem.at[0],
                device_id={'tp': r.partner}, device_id_type=MESH).wait_send()


def scatter_buffers(n, rows, d):
    return [VMEM((n // 2, rows, d), BF), VMEM((3, rows, d), BF), VMEM((3, rows, d), BF)]


def scatter_sems():
    return [pltpu.SemaphoreType.DMA((2,)), pltpu.SemaphoreType.DMA((4 + 6,))]


def hooked(count, body, hooks):
    def step(i):
        for at, actions in hooks.items():
            @pl.when(i == at)
            def _():
                for act in actions:
                    act()
        body(i)
    loop(0, count, step)


def gather_sems():
    return [pltpu.SemaphoreType.DMA((2,)), pltpu.SemaphoreType.DMA((Gather.SLOTS,))]


def lane_mask(rows, h):
    lane = lax.broadcasted_iota(jnp.int32, (rows, 128), 1)
    return (lane < 64) if h == 0 else (lane >= 64)


def attend_block(i, q_ref, k_ref, vt_ref, o_ref, lse_ref, s_ref, m_ref, l_ref, acc_ref, bt_ref, slopes):
    t = q_ref.shape[2]
    e = acc_ref.shape[0] // 2
    key = lax.broadcasted_iota(jnp.int32, (t, t), 0)
    qry = lax.broadcasted_iota(jnp.int32, (t, t), 1)
    for h in PAIR:
        m_ref[h] = jnp.full((8, t), MASK_VALUE, F32)
        l_ref[h] = jnp.zeros((8, t), F32)
    zero_fill(acc_ref)

    def shift(h, j):
        return slopes[h] * (j * t).astype(F32)

    def score(blocks, diag):
        top = [m_ref[h] for h in PAIR]
        for j in blocks:
            for h in PAIR:
                s = mm(k_ref[j], q_ref[h, i], NT) + bt_ref[h]
                if diag:
                    s = jnp.where(key <= qry, s, MASK_VALUE)
                s_ref[h, j] = s
                top[h] = jnp.maximum(top[h], fold8(s, jnp.maximum) + shift(h, j))
        for h in PAIR:
            m_ref[h] = top[h]

    twos(i, lambda blocks: score(blocks, False))
    score((i,), True)
    top = [jnp.max(m_ref[h], axis=0, keepdims=True) for h in PAIR]

    def denom(j):
        for h in PAIR:
            l_ref[h] = l_ref[h] + fold8(jnp.exp(s_ref[h, j] + (shift(h, j) - top[h])), jnp.add)

    loop(0, i + 1, denom)
    for h in PAIR:
        lse_ref[h, i] = top[h] + jnp.log(col_sum(l_ref[h]))

    def values(blocks):
        for h in PAIR:
            rows = pl.ds(h * e, e)
            total = acc_ref[rows, :]
            for j in blocks:
                p = jnp.exp(s_ref[h, j] + (shift(h, j) - lse_ref[h, i])).astype(BF)
                total = total + mm(vt_ref[j, rows, :], p)
            acc_ref[rows, :] = total

    twos(i + 1, values)
    o_ref[i] = acc_ref[...].T.astype(BF)


def kernel_main(n, scale, n_vec, n_out, x_hbm, dy_hbm, wt_hbm, wo_hbm, wu_hbm, wd_hbm, *refs):
    vec_hbm, (slopes_ref,), refs = refs[:n_vec], refs[n_vec:n_vec + 1], refs[n_vec + 1:]
    results, (h_hbm,), refs = refs[:n_out], refs[n_out:n_out + 1], refs[n_out + 1:]
    vecs, refs = refs[:n_vec], refs[n_vec:]
    run_layer(n, scale, vec_hbm, vecs, results, x_hbm, dy_hbm, wt_hbm, wo_hbm, wu_hbm, wd_hbm, slopes_ref, h_hbm, *refs)


def run_layer(n, scale, vec_hbm, vecs, results, x_hbm, dy_hbm, wt_hbm, wo_hbm, wu_hbm, wd_hbm, slopes_ref, h_hbm,
                xg, xo, dyo, dy, hg, wt, wp, wof, wu, wd, q, k, v, kt, vt, o, lse, orow, s_ref, m_ref, l_ref, acc, bt,
                x1, act, dpre, mid, dom, dqt, dk, dv, d3, small, early, late, part,
                *rest):
    g1, b1, bqkv, bo, g2, b2, bu, bd = vecs
    y, gx, sums, gwt, gbq, gwo, gwu, gbu, gwd = results
    rest = list(rest)

    def take(count):
        head = rest[:count]
        del rest[:count]
        return head

    ring = Ring(n)
    me = ring.me
    t, d, f = xg.shape[1], xg.shape[2], wu.shape[1]
    rs_bufs, rm_bufs = take(3), take(3)
    st = t // 2
    streams = (0, st)
    r_sems = [take(2) for _ in PAIR]
    r0, r1 = [Scatter(ring, part, *rs_bufs, *sems, base=base, size=st) for base, sems in zip(streams, r_sems)]
    rs = Scatter(ring, part, *rs_bufs, *r_sems[0])
    rm = Scatter(ring, dy, *rm_bufs, *take(2))
    g_sems = [take(2) for _ in PAIR]
    ax, aw = [Gather(ring, buf, *sems) for buf, sems in zip((xg, wof), g_sems)]
    ay = Gather(ring, dy, *take(2))
    g0, g1s = [Gather(ring, hg, *sems, base=base, size=st) for base, sems in zip(streams, g_sems)]
    d0, d1 = [Gather(ring, xg, *sems, base=base, size=st) for base, sems in zip(streams, g_sems)]
    few, local, vec_sem = take(3)
    o_send, o_recv, e_send, e_recv, l_send, l_recv = [few.at[i] for i in range(6)]

    def fetch(i, src, dst):
        cp = pltpu.make_async_copy(src, dst, local.at[i])
        cp.start()
        return cp

    in_x, in_wo, in_dy, in_wt = (fetch(0, x_hbm, xg.at[me]), fetch(1, wo_hbm, wof.at[me]),
                                 fetch(2, dy_hbm, dy.at[me]), fetch(3, wt_hbm, wt))
    later = [fetch(4, wu_hbm, wu), fetch(5, wd_hbm, wd), fetch(6, x_hbm, xo), fetch(7, dy_hbm, dyo)]
    vec_in = [pltpu.make_async_copy(a, b, vec_sem.at[i]) for i, (a, b) in enumerate(zip(vec_hbm, vecs))]
    for cp in vec_in:
        cp.start()
    ring.barrier()
    in_x.wait()
    ax.start()
    for cp in vec_in:
        cp.wait()
    in_wt.wait()
    sort_weight(wp, wt)
    in_wo.wait()
    in_dy.wait()
    bias = jnp.concatenate([bqkv[kind, head:head + 1, :] for kind in TRIPLE for head in PAIR], axis=1)

    def project(blk):
        def norm(rows):
            hat, _ = norm_rows(xg[blk, rows, :].astype(F32))
            hg[blk, rows, :] = (hat * g1[...] + b1[...]).astype(BF)
        rows_loop(t, 64, norm)
        out = mm(hg[blk], wp[...], NT) + bias
        out = out.astype(BF)
        zero = jnp.zeros((t, 128), BF)
        qs = (out[:, :128].astype(F32) * scale).astype(BF)
        for head in PAIR:
            q[head, blk] = jnp.where(lane_mask(t, head), qs, zero)
        k[blk] = out[:, 128:256]
        v[blk] = out[:, 256:]
        kt[blk] = out[:, 128:256].T
        vt[blk] = out[:, 256:].T
        fetch(0, hg.at[blk], h_hbm.at[blk])

    arrive = functools.partial
    with scope('a_gather'):
        hooked(n, lambda step: project(ring.order(step)), {
            1: [arrive(ax.side, 0)],
            2: [ax.near1, ax.near2],
            4: [arrive(ax.side, 1)],
            5: [arrive(ax.side, 2)],
            6: [ax.drain, aw.start, ax.far, ay.start],
            7: [arrive(ax.side, 3)]})
    slopes = [slopes_ref[me * 2 + head] for head in PAIR]
    key = lax.broadcasted_iota(jnp.int32, (t, t), 0)
    qry = lax.broadcasted_iota(jnp.int32, (t, t), 1)
    for head in PAIR:
        bt[head] = slopes[head] * key.astype(F32)

    def send_o(i):
        cols = pl.ds(pl.multiple_of(me * 128, 128), 128)
        return pltpu.make_async_remote_copy(
            src_ref=o.at[i], dst_ref=orow.at[:, cols], send_sem=o_send, recv_sem=o_recv,
            device_id={'tp': i}, device_id_type=MESH)

    def one_block(step):
        i = ring.order(n - 1 - step)
        attend_block(i, q, k, vt, o, lse, s_ref, m_ref, l_ref, acc, bt, slopes)

        @pl.when(step < n - 1)
        def _():
            send_o(i).start()

    with scope('a_attend'):
        ax.finish()
        pltpu.make_async_copy(hg, h_hbm, local.at[0]).wait()
        hooked(n, one_block, {4: [aw.near1], 5: [aw.near2]})
    most = pl.ds(0, n - 1)
    with scope('a_wait'):
        aw.far()
        ay.near1()
        orow[:, pl.ds(pl.multiple_of(me * 128, 128), 128)] = o[me]
        wide = orow.at[:, pl.ds(0, (n - 1) * 128)]
        pltpu.make_async_remote_copy(
            src_ref=wide, dst_ref=wide, send_sem=o_send, recv_sem=o_recv,
            device_id={'tp': me}, device_id_type=MESH).wait_recv()
        for which in range(4):
            aw.side(which)
        aw.finish()
        later[2].wait()
    with scope('a_out'):
        x1[...] = mm(orow[...], wof[...].reshape(n * 128, d)).astype(BF).astype(F32)

        def enter(rows):
            row = xo[rows, :].astype(F32) + x1[rows, :] + bo[...]
            x1[rows, :] = row
            hat, _ = norm_rows(row)
            hg[me, rows, :] = (hat * g2[...] + b2[...]).astype(BF)
        rows_loop(st, 64, enter)
        g0.start()
        rows_loop(st, 64, enter, base=st)
    for cp in (later[0], later[1], later[3]):
        cp.wait()
    zero_fill(gbu)
    ay.side(0)

    def rest():
        ay.near2()
        ay.far()
        for which in range(1, 4):
            ay.side(which)

    def mlp(blk, stream):
        rows = pl.ds(pl.multiple_of(stream * st, st), st)
        pre = mm(hg[blk, rows, :], wu[...]) + bu[...]
        cot = mm(dy[blk, rows, :], wd[...], NT).astype(BF).astype(F32)
        sq = pre * pre
        th = jnp.tanh(GELU_C * (pre + 0.044715 * sq * pre))
        cdf = 0.5 * (1.0 + th)
        act[blk, rows, :] = (pre * cdf).astype(BF)
        slope = cdf + pre * (0.5 * (1.0 - th * th)) * (GELU_C * (1.0 + 3 * 0.044715 * sq))
        dp = cot * slope
        gbu[...] = gbu[...] + fold8(dp, jnp.add)
        dpb = dp.astype(BF)
        dpre[blk, rows, :] = dpb
        part[blk, rows, :] = mm(dpb, wu[...], NT).astype(BF)

    chips = (ring.xf, ring.xr, ring.xl, ring.x)
    def pairs(job):
        for xp in chips:
            job.send_pair(xp)

    def item(step):
        late = (step == 4) | (step == 5) | (step >= 10)
        pos = jnp.where(step < 4, step, jnp.where(step < 6, step - 4, jnp.where(step < 10, step - 2, step - 8)))
        mlp(ring.order(pos), jnp.where(late, 1, 0))

    with scope('b_gather'):
        hooked(2 * n, item, {
            1: [arrive(g0.side, 0)],
            2: [rest, g0.near1, g1s.start, g0.near2],
            5: [arrive(g1s.side, 0)],
            6: [arrive(g0.side, 1)],
            7: [arrive(g0.side, 2)],
            8: [g0.far],
            9: [arrive(g0.side, 3)],
            10: [arrive(pairs, r0), g1s.near1, r0.far, g1s.near2],
            12: [r0.near_own, arrive(g1s.side, 1)],
            13: [arrive(g1s.side, 2)],
            14: [g1s.far],
            15: [arrive(g1s.side, 3)]})
    with scope('b_far'):
        pairs(r1)
        r0.near_sum()
        r1.far()
    with scope('b_own'):
        r1.near_own()
    ay.finish()

    def weight_down(i):
        cols = pl.ds(pl.multiple_of(i * 256, 256), 256)
        left = act[:, :, cols].reshape(n * t, 256)
        gwd[cols, :] = mm(left, dy[...].reshape(n * t, d), T0).astype(BF)

    def weight_up(i):
        cols = pl.ds(pl.multiple_of(i * 256, 256), 256)
        left = hg[:, :, cols].reshape(n * t, 256)
        gwu[cols, :] = mm(left, dpre[...].reshape(n * t, f), T0).astype(BF)

    with scope('b_weights'):
        loop(0, f // 256, weight_down)
        loop(0, d // 256, weight_up)
    zero_fill(small)

    def down(blk):
        dy[blk] = mm(act[blk], wd[...]).astype(BF)

    def leave(rows):
        dg = rs.total(rows).astype(BF).astype(F32)
        hat, rstd = norm_rows(x1[rows, :])
        small[2] = small[2] + fold8(dg * hat, jnp.add)
        small[3] = small[3] + fold8(dg, jnp.add)
        dz = norm_back(dg * g2[...], hat, rstd)
        dyf = dyo[rows, :].astype(F32)
        dm = dyf + dz
        small[4] = small[4] + fold8(dm, jnp.add)
        small[5] = small[5] + fold8(dyf, jnp.add)
        mid[rows, :] = dm
        xg[me, rows, :] = dm.astype(BF)

    with scope('b_sum'):
        r1.near_sum()
    with scope('b_final'):
        r0.wait_final()
    with scope('b_leave'):
        rows_loop(st, 64, leave)
        g0.finish()
        d0.start()
    with scope('b_down'):
        loop(0, n, down)
        pairs(rm)
    with scope('b_final1'):
        r1.wait_final()
    with scope('b_leave1'):
        rows_loop(st, 64, leave, base=st)
        g1s.finish()
        d1.start()
    with scope('b_finish'):
        for job in (r0, r1):
            job.finish()
    reload = fetch(0, h_hbm, hg)

    def share(buf, off, send_sem, recv_sem):
        return pltpu.make_async_remote_copy(
            src_ref=buf.at[me], dst_ref=buf.at[me], send_sem=send_sem, recv_sem=recv_sem,
            device_id={'tp': (me + off) % n}, device_id_type=MESH)

    def all_in(buf, send_sem, recv_sem):
        return pltpu.make_async_remote_copy(
            src_ref=buf.at[most], dst_ref=buf.at[most], send_sem=send_sem, recv_sem=recv_sem,
            device_id={'tp': me}, device_id_type=MESH)

    def early_out():
        for i in range(4):
            early[me, i:i + 1, :] = col_sum(small[2 + i])
        for off in range(1, n):
            share(early, off, e_send, e_recv).start()

    def add_up(buf):
        total = buf[0]
        for b in range(1, n):
            total = total + buf[b]
        return total
    zero_fill(dk, dv)

    def back_block(i):
        dc = mm(xg[i], wof[me], NT).astype(BF)
        zero = jnp.zeros((t, 128), BF)
        prod = (dc.astype(F32) * o[i].astype(F32)).T
        dlt = (col_sum(prod[:64]), col_sum(prod[64:]))
        for head in PAIR:
            dom[head] = jnp.where(lane_mask(t, head), dc, zero)
        zero_fill(dqt)

        def pair_block(blocks, diag):
            cases = [(j, head) for j in blocks for head in PAIR]
            ps, dss = [], []
            for j, head in cases:
                s = mm(k[j], q[head, i], NT) + bt[head]
                if diag:
                    s = jnp.where(key <= qry, s, MASK_VALUE)
                p = jnp.exp(s + (slopes[head] * (j * t).astype(F32) - lse[head, i]))
                dp = mm(v[j], dom[head], NT).astype(BF).astype(F32)
                dss.append((p * (dp - dlt[head])).astype(BF))
                ps.append(p.astype(BF))
            wide = list(zip(cases, ps, dss))
            for j in blocks:
                dv[j] = dv[j] + sum(mm(p, dom[head]) for (b, head), p, _ in wide if b is j)
                dk[j] = dk[j] + sum(mm(ds, q[head, i]) for (b, head), _, ds in wide if b is j)
            for head in PAIR:
                rows = pl.ds(head * 64, 64)
                dqt[rows, :] = dqt[rows, :] + sum(mm(kt[b, rows, :], ds) for (b, h), _, ds in wide if h == head)

        twos(i, lambda blocks: pair_block(blocks, False))
        pair_block((i,), True)
        d3[i, :, :128] = (dqt[...].T * scale).astype(BF)

    def both_in(which):
        for job in (d0, d1):
            job.side(which)

    with scope('c_attend'):
        hooked(n, lambda step: back_block(ring.order(step)), {
            1: [arrive(both_in, 0), d0.near1, d0.near2],
            2: [d1.near1, rm.far, rm.near_own, d1.near2],
            4: [arrive(both_in, 1)],
            5: [arrive(both_in, 2)],
            6: [d0.far, d1.far, rm.near_sum],
            7: [arrive(both_in, 3)]})
    zero_fill(gbq)

    def back_in(xp):
        for off in (1, 0):
            blk = xp * 2 + (ring.c + off) % 2
            d3[blk, :, 128:256] = dk[blk].astype(BF)
            d3[blk, :, 256:] = dv[blk].astype(BF)
            part[blk] = mm(d3[blk], wp[...]).astype(BF)
            if off:
                rs.send_pair(xp)

    with scope('c_far'):
        back_in(ring.xf)
        rs.far()
    with scope('c_own'):
        back_in(ring.xr)
        back_in(ring.xl)
        rs.near_own()
        back_in(ring.x)
    reload.wait()

    def weight_in(i):
        cols = pl.ds(pl.multiple_of(i * 128, 128), 128)
        left = d3[:, :, cols].reshape(n * t, 128)
        grad = mm(left, hg[...].reshape(n * t, d), T0).astype(BF)
        for head in PAIR:
            gwt[head, i] = grad[head * 64:head * 64 + 64]

    def bias_in(b):
        gbq[...] = gbq[...] + fold8(d3[b].astype(F32), jnp.add)

    with scope('c_weights'):
        loop(0, len(TRIPLE), weight_in)
        loop(0, n, bias_in)
    with scope('c_sum'):
        rs.near_sum()
    with scope('c_gwo'):
        gwo[...] = mm(o[...].reshape(n * t, 128), xg[...].reshape(n * t, d), T0).astype(BF)
    with scope('c_mfinal'):
        rm.wait_final()

    def finish_y(rows):
        m = rm.total(rows).astype(BF).astype(F32)
        y[rows, :] = (x1[rows, :] + m + bd[...]).astype(BF)
    rows_loop(t, 64, finish_y)
    with scope('c_final'):
        rs.wait_final()
        early_out()

    def sum_in(rows):
        dh = rs.total(rows).astype(BF).astype(F32)
        hat, _ = norm_rows(xo[rows, :].astype(F32))
        small[0] = small[0] + fold8(dh * hat, jnp.add)
        small[1] = small[1] + fold8(dh, jnp.add)

    def last(rows):
        dh = rs.total(rows).astype(BF).astype(F32)
        hat, rstd = norm_rows(xo[rows, :].astype(F32))
        gx[rows, :] = (mid[rows, :] + norm_back(dh * g1[...], hat, rstd)).astype(BF)

    with scope('c_sums'):
        rows_loop(t, 64, sum_in)
    for i in PAIR:
        late[me, i:i + 1, :] = col_sum(small[i])
    with scope('c_share'):
        for off in range(1, n):
            share(late, off, l_send, l_recv).start()
        rows_loop(t, 64, last)
        all_in(early, e_send, e_recv).wait_recv()
        sums[2:6, :] = add_up(early)
        all_in(late, l_send, l_recv).wait_recv()
        sums[0:2, :] = add_up(late)
        all_in(early, e_send, e_recv).wait_send()
        all_in(late, l_send, l_recv).wait_send()
        all_in(o, o_send, o_recv).wait_send()
    with scope('d_finish'):
        for job in (rs, rm, d0, d1):
            job.finish()


def kernel_out(n_big, *refs):
    count = n_big + 3
    srcs, refs = refs[:count], refs[count:]
    outs, refs = refs[:n_big + 8], refs[n_big + 8:]
    bufs, tail, sem_out = srcs, refs[:-1], refs[-1]
    gbq, gbu, sums = bufs[n_big:]
    o_bq, o_bu, o_sums = tail
    kept = list(bufs[:n_big]) + [o_bq, o_bu] + [o_sums.at[i:i + 1] for i in range(6)]
    backs = [pltpu.make_async_copy(b, a, sem_out.at[i]) for i, (a, b) in enumerate(zip(outs, kept))]
    for back in backs[:n_big]:
        back.start()
    o_bu[...] = col_sum(gbu[...])
    row = col_sum(gbq[...])
    e = o_bq.shape[2]
    for part_no in TRIPLE:
        for head in PAIR:
            at = (part_no * 2 + head) * e
            o_bq[part_no, head:head + 1, :] = row[:, at:at + e]
    o_sums[...] = sums[...]
    for back in backs[n_big:]:
        back.start()
    for back in backs:
        back.wait()


def inside():
    return pl.BlockSpec(memory_space=VMEM)


def anywhere():
    return pl.BlockSpec(memory_space=pl.ANY)


def smem():
    return pl.BlockSpec(memory_space=pltpu.SMEM)


def solution(mesh):
    n = mesh.shape['tp']

    def local_step(x, ln1_gamma, ln1_beta, w_qkv, b_qkv, w_out, b_out, ln2_gamma, ln2_beta, w_up, b_up, w_down, b_down, grad_y):
        t, d = x.shape[1], x.shape[2]
        heads, e = w_qkv.shape[1], w_qkv.shape[3]
        he = heads * e
        f = w_up.shape[1]
        scale = e ** -0.5
        slopes = jnp.asarray(alibi_slopes(heads * n))
        x2, dy2 = x[0], grad_y[0]
        row = lambda vec: vec.reshape(1, -1)
        wt = w_qkv.transpose(1, 2, 3, 0).reshape(heads * 3 * e, d)
        bq = b_qkv.transpose(1, 0, 2)
        sds = jax.ShapeDtypeStruct
        rows, full, half = (t, d), (n, t, d), (n, t, he)
        both, line = (len(PAIR),) + half, (len(PAIR), n, 1, t)
        packed = (len(TRIPLE) * he, d)
        params = lambda cid: pltpu.CompilerParams(collective_id=cid, has_side_effects=True, vmem_limit_bytes=VLIM)
        dma = pltpu.SemaphoreType.DMA

        vm = lambda dims, kind=BF: VMEM(dims, kind)
        stat, turned = (len(PAIR), 8, t), (n, he, t)
        vecs = (row(ln1_gamma), row(ln1_beta), bq, row(b_out), row(ln2_gamma), row(ln2_beta), row(b_up), row(b_down))
        results = [sds(rows, BF), sds(rows, BF), sds((8, d), F32), sds((heads, len(TRIPLE), e, d), BF),
                   sds((8, len(TRIPLE) * he), F32), sds((he, d), BF), sds((d, f), BF), sds((8, f), F32), sds((f, d), BF)]
        y, gx, sums, gwt, gbq, gwo, gwu, gbu, gwd, _ = pl.pallas_call(
            functools.partial(kernel_main, n, scale, len(vecs), len(results)),
            name='layer',
            out_shape=[vm(b.shape, b.dtype) for b in results] + [sds(full, BF)],
            in_specs=[anywhere()] * (6 + len(vecs)) + [smem()],
            out_specs=[inside()] * len(results) + [anywhere()],
            scratch_shapes=[vm(b.shape, b.dtype) for b in vecs] + [vm(full), vm(rows), vm(rows), vm(full), vm(full), vm(packed), vm(packed), vm((n, he, d)),
                            vm((d, f)), vm((f, d)), vm(both), vm(half), vm(half), vm(turned), vm(turned), vm(half),
                            vm(line, F32), vm(rows), vm((len(PAIR), n, t, t), F32), vm(stat, F32), vm(stat, F32),
                            vm((he, t), F32), vm((len(PAIR), t, t), F32), vm(rows, F32), vm((n, t, f)), vm((n, t, f)),
                            vm(rows, F32), vm((len(PAIR), t, he)), vm((he, t), F32), vm(half, F32), vm(half, F32),
                            vm((n, t, len(TRIPLE) * he)), vm((6, 8, d), F32), vm((n, 4, d), F32), vm((n, 2, d), F32), vm(full)]
            + scatter_buffers(n, t, d) * 2 + scatter_sems() * 3 + gather_sems() * 3 + [dma((n,))] * 2 + [dma((len(vecs),))],
            compiler_params=params(0),
        )(x2, dy2, wt, w_out, w_up, w_down, *vecs, slopes)

        big = (y, gx, gwt, gwo, gwu, gwd)
        little = (gbq, gbu, sums)
        bias_dims, up_dims = (len(TRIPLE), heads, e), (1, f)
        res = pl.pallas_call(
            functools.partial(kernel_out, len(big)),
            name='results',
            compiler_params=pltpu.CompilerParams(vmem_limit_bytes=8 * 1024 * 1024),
            out_shape=[sds(b.shape, b.dtype) for b in big] + [sds(bias_dims, F32), sds(up_dims, F32)] + [sds((1, d), F32)] * 6,
            in_specs=[inside()] * (len(big) + 3),
            out_specs=[anywhere()] * (len(big) + 8),
            scratch_shapes=[vm(bias_dims, F32), vm(up_dims, F32), vm((8, d), F32), dma((len(big) + 8,))],
        )(*big, *little)
        y, gx, gwt, gwo, gwu, gwd, gbq, gbu, s_g1, s_b1, s_g2, s_b2, s_bo, s_bd = res
        vec = lambda a: a.reshape(-1)
        return (y[None], gx[None], vec(s_g1), vec(s_b1), gwt.transpose(3, 0, 1, 2), gbq.transpose(1, 0, 2), gwo, vec(s_bo),
                vec(s_g2), vec(s_b2), gwu, vec(gbu), gwd, vec(s_bd))

    row_spec = P('dp', 'tp', None)
    in_specs = (row_spec, P(), P(), P(None, 'tp', None, None), P('tp', None, None), P('tp', None), P(), P(), P(),
                P(None, 'tp'), P('tp'), P('tp', None), P(), row_spec)
    out_specs = (row_spec, row_spec, P('dp'), P('dp'), P('dp', 'tp', None, None), P(('dp', 'tp'), None, None),
                 P(('dp', 'tp'), None), P('dp'), P('dp'), P('dp'), P('dp', 'tp'), P(('dp', 'tp')), P(('dp', 'tp'), None), P('dp'))
    return jax.shard_map(local_step, mesh=mesh, in_specs=in_specs, out_specs=out_specs, check_vma=False)
```

profile of v0, /device:TPU:81, one launch (start us, length us, event | category | flops | bytes accessed | tf_op | source)
XLA Modules:
  0.0 154.0 jit_solution(2138205802343412141)
XLA Ops:
  0.7 151.0 %layer.1 = (bf16[256,1024]{1,0:T(8,128)(2,1)S(1)}, bf16[256,1024]{1,0:T(8,128)(2,1)S(1)}, f32[8,1024]{1,0:T(8,128)S(1)}, bf16[2,3,64,1024]{3,2,1,0:T(8,128)(2,1)...) custom-call(bf16[256,1024]{1,0:T(8,128)(2,1)} %bitcast.25, ...), custom_call_target="tpu_custom_call" | custom-call | tf_op jit(solution)/shard_map/layer/pallas_call | solution.py:828
  151.6 2.2 %results.1 = (bf16[256,1024]{1,0:T(8,128)(2,1)}, bf16[256,1024]{1,0:T(8,128)(2,1)}, bf16[2,3,64,1024]{3,2,1,0:T(8,128)(2,1)}, bf16[128,1024]{1,0:T(8,128)(2,1)},...) custom-call(bf16[256,1024]{1,0:T(8,128)(2,1)S(1)} %get-tuple-element, ...), custom_call_target="tpu_custom_call" | custom-call | tf_op jit(solution)/shard_map/results/pallas_call | solution.py:847
where the time goes:
time: 154 us
  Pallas kernels  153 us (99%)
    pallas_call x1, Pallas kernels, local_step(): pl.pallas_call(functools.partial(kernel_main, n, scale, len(vecs), len(re...  151 us

commit v1 on v0

--- a/solution.py
+++ b/solution.py
@@ -553,10 +553,9 @@
             12: [r0.near_own, arrive(g1s.side, 1)],
             13: [arrive(g1s.side, 2)],
             14: [g1s.far],
-            15: [arrive(g1s.side, 3)]})
+            15: [arrive(g1s.side, 3), r0.near_sum]})
     with scope('b_far'):
         pairs(r1)
-        r0.near_sum()
         r1.far()
     with scope('b_own'):
         r1.near_own()

time: 154 us -> 155 us (level)
  no operation moved by 1% of the time
where the time goes in v1:
time: 155 us; the launch traced here: 154 us
  Pallas kernels  154 us (99%)
    pallas_call x1, Pallas kernels, local_step(): pl.pallas_call(functools.partial(kernel_main, n, scale, len(vecs), len(re...  152 us

profile of v1, /device:TPU:81, one launch (start us, length us, event | category | flops | bytes accessed | tf_op | source)
XLA Modules:
  0.0 154.5 jit_solution(4811148540828956747)
XLA Ops:
  0.7 151.5 %layer.1 = (bf16[256,1024]{1,0:T(8,128)(2,1)S(1)}, bf16[256,1024]{1,0:T(8,128)(2,1)S(1)}, f32[8,1024]{1,0:T(8,128)S(1)}, bf16[2,3,64,1024]{3,2,1,0:T(8,128)(2,1)...) custom-call(bf16[256,1024]{1,0:T(8,128)(2,1)} %bitcast.25, ...), custom_call_target="tpu_custom_call" | custom-call | tf_op jit(solution)/shard_map/layer/pallas_call | solution.py:827
  152.2 2.2 %results.1 = (bf16[256,1024]{1,0:T(8,128)(2,1)}, bf16[256,1024]{1,0:T(8,128)(2,1)}, bf16[2,3,64,1024]{3,2,1,0:T(8,128)(2,1)}, bf16[128,1024]{1,0:T(8,128)(2,1)},...) custom-call(bf16[256,1024]{1,0:T(8,128)(2,1)S(1)} %get-tuple-element, ...), custom_call_target="tpu_custom_call" | custom-call | tf_op jit(solution)/shard_map/results/pallas_call | solution.py:846
